TPU v7x, 128 devices: a whole 4x4x4 slice. The times are simulated.
128 devices in a mesh: gx: 16 (over y, z), gy: 8 (over x, core).
Axes of the slice: x: 4, y: 4, z: 4, core: 2. Of those that a mesh axis runs over, the one named last changes fastest.
Arguments:
- velocity: float32 [3, 128, 512, 384], P(None, 'gx', 'gy')
- target_profile: float32 [2, 384], replicated, may hold values from 0.5 to 1.5
- disc_turbine: int32 [128, 4], P(('gx', 'gy')), may hold values from -1 to 99, as said below
- disc_start: int32 [3, 128, 4], P(None, ('gx', 'gy')), may hold values from 0 to 256, as said below
- disc_weight: float32 [128, 4, 16, 128], P(('gx', 'gy')), may hold values from 0.2 to 1
- turbine_owner: int32 [100], replicated, may hold values from 0 to 127, as said below
- mode_flag: int32 [100], replicated, may hold values from 0 to 2
- controller_state: float32 [128, 4], P(('gx', 'gy')), may hold values from -4 to 4
Outputs:
- advanced_velocity: float32 [3, 128, 512, 384], P(None, 'gx', 'gy')
- profiles: float32 [4, 384], replicated
- thrust_setpoint: float32 [100], replicated
- controller_next: float32 [128, 4], P(('gx', 'gy'))
Inputs may be any that keep to these rules, and one draw needn't show every extreme that they name: `disc_turbine`: -1 marks an empty slot; every turbine number appears in at least one slot; some device has all 4 slots filled. `disc_start`: row 0 is a cell of the device's block along the first dimension, 0 to 7; row 1 the first of 16 cells along the second, 0 to 48; row 2 the first of 128 heights, 0 to 256. `turbine_owner`: no device owns more than 4 turbines, and some device owns exactly 4.
All inputs are finite; a program needn't handle non-finite values.
Results may differ from a plain program's by a relative error of at most 0.00013.
Values sent between devices are 32-bit elements; how exact they have to be, the bound alone decides.
No kernel may reach another device: no remote copies, remote signals or barrier semaphores. Data moves between devices by JAX's collectives and lax.ppermute only.
A program may use at most 128 MiB of HBM per device.

v0:
```python
import jax
import jax.numpy as jnp
from jax import lax
from jax.sharding import Mesh
from jax.sharding import PartitionSpec as P

STEPS = 4
GX = ("gx_0", "gx_1")
GY = ("gy_0", "gy_1")
GX_GY = ("gx_0", "gx_1", "gy_0", "gy_1")
VISCOSITY = 0.1
TIME_STEP = 0.2
RELAX_TIME = 2.0
CONTROL_STEP = 0.5
GAIN_PROPORTIONAL = 2.0
GAIN_INTEGRAL = 1.0
HIGHEST = lax.Precision.HIGHEST


def by_axis(shard, axes):
    for axis in axes:
        shard = lax.psum(shard, axis)
    return shard


def padded_2(shard, sides, width):
    edges = {}
    for axis, dim in sides:
        size, length = (lax.axis_size(axis), shard.shape[dim])
        up = [(i, (i + 1) % size) for i in range(size)]
        last = lax.slice_in_dim(shard, length - width, length, axis=dim)
        first = lax.slice_in_dim(shard, 0, width, axis=dim)
        edges[dim] = (
            lax.ppermute(last, axis, up),
            lax.ppermute(first, axis, [(b, a) for a, b in up]),
        )
    done = []
    for _, dim in sides:
        low, high = edges[dim]
        around = [(width, width) if d in done else (0, 0) for d in range(shard.ndim)]
        shard = jnp.concatenate([jnp.pad(low, around), shard, jnp.pad(high, around)], axis=dim)
        done.append(dim)
    return shard


def pad_height(block):
    return jnp.pad(block, ((0, 0), (0, 0), (0, 0), (2, 2)))


def tendency(block):
    length_x = block.shape[1] - 4
    length_y = block.shape[2] - 4
    length_z = block.shape[3] - 4

    def shifted(offset_x, offset_y, offset_z):
        return block[
            :,
            2 + offset_x : 2 + offset_x + length_x,
            2 + offset_y : 2 + offset_y + length_y,
            2 + offset_z : 2 + offset_z + length_z,
        ]

    centre = shifted(0, 0, 0)
    grad_x = (
        8.0 * (shifted(1, 0, 0) - shifted(-1, 0, 0)) - (shifted(2, 0, 0) - shifted(-2, 0, 0))
    ) / 12.0
    grad_y = (
        8.0 * (shifted(0, 1, 0) - shifted(0, -1, 0)) - (shifted(0, 2, 0) - shifted(0, -2, 0))
    ) / 12.0
    grad_z = (
        8.0 * (shifted(0, 0, 1) - shifted(0, 0, -1)) - (shifted(0, 0, 2) - shifted(0, 0, -2))
    ) / 12.0
    laplacian = (
        shifted(1, 0, 0)
        + shifted(-1, 0, 0)
        + (shifted(0, 1, 0) + shifted(0, -1, 0))
        + (shifted(0, 0, 1) + shifted(0, 0, -1))
        - 6.0 * centre
    )
    advection = centre[0:1] * grad_x + centre[1:2] * grad_y + centre[2:3] * grad_z
    return VISCOSITY * laplacian - advection


def control_terms(mode_flag):
    rated_speed = jnp.where(mode_flag == 0, 0.7, jnp.where(mode_flag == 1, 0.9, 1.1)).astype(
        jnp.float32
    )
    bias_terms = jnp.where(mode_flag == 0, 1.0, jnp.where(mode_flag == 1, 0.0, -1.0)).astype(
        jnp.float32
    )
    return (rated_speed, bias_terms)


def owner_rank(turbine_owner):
    turbines = turbine_owner.shape[0]
    same_owner = turbine_owner[:, None] == turbine_owner[None, :]
    earlier = (
        jnp.arange(turbines, dtype=jnp.int32)[None, :]
        < jnp.arange(turbines, dtype=jnp.int32)[:, None]
    )
    return jnp.sum((same_owner & earlier).astype(jnp.int32), axis=1)


def thrust_from(bias_terms, speed_error, integral):
    return 0.1 + 0.9 * jax.nn.sigmoid(
        bias_terms - GAIN_PROPORTIONAL * speed_error - GAIN_INTEGRAL * integral
    )


def local(
    velocity,
    target_profile,
    disc_turbine,
    disc_start,
    disc_weight,
    turbine_owner,
    mode_flag,
    controller_state,
):
    blocks_x = lax.axis_size(GX)
    blocks_y = lax.axis_size(GY)
    devices = blocks_x * blocks_y
    device_me = lax.axis_index(GX) * blocks_y + lax.axis_index(GY)
    length_x = velocity.shape[1]
    length_y = velocity.shape[2]
    length_z = velocity.shape[3]
    turbines = mode_flag.shape[0]
    owned = controller_state.shape[1]
    slots = disc_turbine.shape[1]
    tile_y = disc_weight.shape[2]
    tile_z = disc_weight.shape[3]
    weights_local = disc_weight[0]
    start_x = disc_start[0, 0]
    start_y = disc_start[1, 0]
    start_z = disc_start[2, 0]
    turbine_ids = jnp.arange(turbines, dtype=jnp.int32)
    slot_onehot = (disc_turbine[0][:, None] == turbine_ids[None, :]).astype(jnp.float32)
    area_part = jnp.dot(jnp.sum(weights_local, axis=(1, 2)), slot_onehot, precision=HIGHEST)
    disc_area = by_axis(area_part, GX_GY)
    owner_slot = owner_rank(turbine_owner)
    owner_column = turbine_owner * owned + owner_slot
    pick_table = (
        owner_column[:, None] == jnp.arange(devices * owned, dtype=jnp.int32)[None, :]
    ).astype(jnp.float32)
    mine_table = (
        (turbine_owner[:, None] == device_me)
        & (owner_slot[:, None] == jnp.arange(owned, dtype=jnp.int32)[None, :])
    ).astype(jnp.float32)
    live_slot = jnp.sum(mine_table, axis=0)
    rated_speed, bias_terms = control_terms(mode_flag)
    integral = controller_state[0]
    state_all = lax.all_gather(controller_state[0], GX_GY, axis=0, tiled=True)
    integral_all = jnp.dot(pick_table, state_all, precision=HIGHEST)
    plane_cells = float(length_x * blocks_x * length_y * blocks_y)
    profiles = jnp.zeros((4, length_z), jnp.float32)
    thrust = jnp.zeros((turbines,), jnp.float32)
    for turn_index in range(STEPS):
        streamwise = velocity[0]
        contribution = jnp.stack(
            [
                jnp.sum(
                    weights_local[slot_index]
                    * lax.dynamic_slice(
                        streamwise,
                        (start_x[slot_index], start_y[slot_index], start_z[slot_index]),
                        (1, tile_y, tile_z),
                    )[0]
                )
                for slot_index in range(slots)
            ]
        )
        numerator_part = jnp.dot(contribution, slot_onehot, precision=HIGHEST)
        plane_part = jnp.stack(
            [
                jnp.sum(velocity[0], axis=(0, 1)),
                jnp.sum(velocity[1], axis=(0, 1)),
                jnp.sum(velocity[2], axis=(0, 1)),
                jnp.sum(velocity[0] * velocity[2], axis=(0, 1)),
            ]
        )
        plane_sums, numerator = (by_axis(plane_part, GX_GY), by_axis(numerator_part, GX_GY))
        disc_speed = numerator / disc_area
        speed_error = disc_speed - rated_speed
        integral_all = integral_all + CONTROL_STEP * speed_error
        thrust = thrust_from(bias_terms, speed_error, integral_all)
        thrust_factor = 0.5 * thrust * disc_speed * jnp.abs(disc_speed)
        slot_factor = jnp.dot(slot_onehot, thrust_factor, precision=HIGHEST)
        force_field = jnp.zeros((length_x, length_y, length_z), jnp.float32)
        for slot_index in range(slots):
            corner = (start_x[slot_index], start_y[slot_index], start_z[slot_index])
            previous = lax.dynamic_slice(force_field, corner, (1, tile_y, tile_z))
            force_field = lax.dynamic_update_slice(
                force_field,
                previous - slot_factor[slot_index] * weights_local[slot_index][None],
                corner,
            )
        plane_means = plane_sums / plane_cells
        profiles = profiles + jnp.stack(
            [
                plane_means[0],
                plane_means[1],
                plane_means[2],
                plane_means[3] - plane_means[0] * plane_means[2],
            ]
        )
        nudging = (target_profile - plane_means[0:2]) / RELAX_TIME
        padded = padded_2(velocity, ((GX, 1), (GY, 2)), 2)
        changes = tendency(pad_height(padded))
        velocity = jnp.stack(
            [
                velocity[0] + TIME_STEP * (changes[0] + nudging[0][None, None, :] + force_field),
                velocity[1] + TIME_STEP * (changes[1] + nudging[1][None, None, :]),
                velocity[2] + TIME_STEP * changes[2],
            ]
        )
    integral = jnp.dot(integral_all, mine_table, precision=HIGHEST) + (1.0 - live_slot) * integral
    return (velocity, profiles / STEPS, thrust, integral[None, :])


def solution(mesh):
    torus = Mesh(mesh.devices.reshape(4, 4, 4, 2), ("gx_0", "gx_1", "gy_0", "gy_1"))
    placed = (
        P(None, GX, GY, None),
        P(),
        P(GX_GY, None),
        P(None, GX_GY, None),
        P(GX_GY, None, None, None),
        P(),
        P(),
        P(GX_GY, None),
    )
    return jax.shard_map(
        local,
        mesh=torus,
        in_specs=placed,
        out_specs=(P(None, GX, GY, None), P(), P(), P(GX_GY, None)),
        check_vma=False,
    )
```

profile of v0, /device:TPU:1, one launch (start us, length us, event | category | flops | bytes accessed | tf_op | source)
XLA Modules:
  0.0 434.5 jit_solution(4336565369596881345)
XLA Ops:
  42.4 6.9 %all-reduce.24 = (f32[4,384]{1,0:T(4,128)S(1)}, f32[100]{0:T(128)S(1)}, f32[100]{0:T(128)S(1)}) all-reduce(f32[4,384]{1,0:T(4,128)S(1)} %pad_maximum_fusion.12, f32[100]{0:T(128)S(1)} %convolution_bitcast_fusion.10, f32[100]{0:T(128)S(1)} %convolution_bitcast_fusion.9), channel_id=1, replica_groups=mesh['gx_0'=4,'gx_1'=4,'gy_0'=4,'gy_1'=2] {'gx_0'}, use_global_device_ids=true, to_apply=%region_4.0 | all-reduce | flops 1736 | bytes 13888 | tf_op jit(solution)/shard_map/psum | solution.py:22
  49.3 7.3 %all-reduce.20 = (f32[4,384]{1,0:T(4,128)S(1)}, f32[100]{0:T(128)S(1)}, f32[100]{0:T(128)S(1)}) all-reduce(f32[4,384]{1,0:T(4,128)S(1)} %get-tuple-element.65, f32[100]{0:T(128)S(1)} %get-tuple-element.66, f32[100]{0:T(128)S(1)} %get-tuple-element.67), channel_id=1, replica_groups=mesh['gx_0'=4,'gx_1'=4,'gy_0'=4,'gy_1'=2] {'gx_1'}, use_global_device_ids=true, to_apply=%region_5.0 | all-reduce | flops 1736 | bytes 13888 | tf_op jit(solution)/shard_map/psum | solution.py:22
  56.6 9.7 %all-reduce.16 = (f32[4,384]{1,0:T(4,128)S(1)}, f32[100]{0:T(128)S(1)}, f32[100]{0:T(128)S(1)}) all-reduce(f32[4,384]{1,0:T(4,128)S(1)} %get-tuple-element.56, f32[100]{0:T(128)S(1)} %get-tuple-element.57, f32[100]{0:T(128)S(1)} %get-tuple-element.58), channel_id=1, replica_groups=mesh['gx_0'=4,'gx_1'=4,'gy_0'=4,'gy_1'=2] {'gy_0'}, use_global_device_ids=true, to_apply=%region_6.0 | all-reduce | flops 1736 | bytes 13888 | tf_op jit(solution)/shard_map/psum | solution.py:22
  66.4 6.2 %all-reduce.28 = (f32[4,384]{1,0:T(4,128)S(1)}, f32[100]{0:T(128)S(1)}, f32[100]{0:T(128)S(1)}) all-reduce(f32[4,384]{1,0:T(4,128)S(1)} %get-tuple-element.47, f32[100]{0:T(128)S(1)} %get-tuple-element.48, f32[100]{0:T(128)S(1)} %get-tuple-element.49), channel_id=1, replica_groups=mesh['gx_0'=4,'gx_1'=4,'gy_0'=4,'gy_1'=2] {'gy_1'}, use_global_device_ids=true, to_apply=%region_7.8 | all-reduce | flops 1736 | bytes 13888 | tf_op jit(solution)/shard_map/psum | solution.py:22
  73.3 62.9 %all-reduce.12 = f32[512]{0:T(512)S(1)} all-reduce(f32[512]{0:T(512)S(1)} %bitcast_dynamic-update-slice_fusion), channel_id=2, replica_groups=mesh['gx_0'=4,'gx_1'=4,'gy_0'=4,'gy_1'=2] {'gx_0','gx_1','gy_0','gy_1'}, use_global_device_ids=true, to_apply=%add.12 | all-reduce | flops 512 | bytes 4096 | tf_op jit(solution)/shard_map/all_gather | solution.py:152
  151.7 8.2 %fusion.33 = f32[3,8,64,384]{3,2,1,0:T(8,128)S(1)} fusion(f32[3,12,68,388]{3,2,1,0:T(8,128)S(1)} %select_maximum_fusion.18, f32[3,12,64,384]{3,2,1,0:T(8,128)} %copy-done.15, f32[3,12,2,384]{3,2,1,0:T(2,128)} %copy-done.31, f32[3,12,2,384]{3,2,1,0:T(2,128)} %copy-done.30, f32[3,10,64,384]{3,2,1,0:T(8,128)} %copy-done.16, ...), kind=kLoop, calls=%fused_computation.81 | loop fusion | flops 17694720 | bytes 29712384 | tf_op jit(solution)/shard_map/sub | solution.py:81
  168.1 7.0 %all-reduce.23 = (f32[4,384]{1,0:T(4,128)S(1)}, f32[100]{0:T(128)S(1)}) all-reduce(f32[4,384]{1,0:T(4,128)S(1)} %pad_maximum_fusion.13, f32[100]{0:T(128)S(1)} %convolution_bitcast_fusion.6), channel_id=1, replica_groups=mesh['gx_0'=4,'gx_1'=4,'gy_0'=4,'gy_1'=2] {'gx_0'}, use_global_device_ids=true, to_apply=%region_26.27 | all-reduce | flops 1636 | bytes 13088 | tf_op jit(solution)/shard_map/psum | solution.py:22
  175.1 7.8 %all-reduce.19 = (f32[4,384]{1,0:T(4,128)S(1)}, f32[100]{0:T(128)S(1)}) all-reduce(f32[4,384]{1,0:T(4,128)S(1)} %get-tuple-element.63, f32[100]{0:T(128)S(1)} %get-tuple-element.64), channel_id=1, replica_groups=mesh['gx_0'=4,'gx_1'=4,'gy_0'=4,'gy_1'=2] {'gx_1'}, use_global_device_ids=true, to_apply=%region_27.28 | all-reduce | flops 1636 | bytes 13088 | tf_op jit(solution)/shard_map/psum | solution.py:22
  182.9 6.5 %all-reduce.15 = (f32[4,384]{1,0:T(4,128)S(1)}, f32[100]{0:T(128)S(1)}) all-reduce(f32[4,384]{1,0:T(4,128)S(1)} %get-tuple-element.54, f32[100]{0:T(128)S(1)} %get-tuple-element.55), channel_id=1, replica_groups=mesh['gx_0'=4,'gx_1'=4,'gy_0'=4,'gy_1'=2] {'gy_0'}, use_global_device_ids=true, to_apply=%region_28.29 | all-reduce | flops 1636 | bytes 13088 | tf_op jit(solution)/shard_map/psum | solution.py:22
  189.4 8.4 %all-reduce.27 = (f32[4,384]{1,0:T(4,128)S(1)}, f32[100]{0:T(128)S(1)}) all-reduce(f32[4,384]{1,0:T(4,128)S(1)} %get-tuple-element.45, f32[100]{0:T(128)S(1)} %get-tuple-element.46), channel_id=1, replica_groups=mesh['gx_0'=4,'gx_1'=4,'gy_0'=4,'gy_1'=2] {'gy_1'}, use_global_device_ids=true, to_apply=%region_29.30 | all-reduce | flops 1636 | bytes 13088 | tf_op jit(solution)/shard_map/psum | solution.py:22
  220.7 7.7 %select_maximum_fusion.12 = f32[3,12,68,388]{3,2,1,0:T(8,128)S(1)} fusion(f32[3,12,2,384]{3,2,1,0:T(2,128)S(1)} %pad.41, f32[3,12,2,384]{3,2,1,0:T(2,128)S(1)} %pad.42, f32[3,2,64,384]{3,2,1,0:T(8,128)} %collective-permute-done.4, f32[3,2,64,384]{3,2,1,0:T(8,128)} %collective-permute-done.5, f32[1,8,64,384]{3,2,1,0:T(8,128)S(1)} %copy-done.11, ...), kind=kLoop, calls=%fused_computation.14 | loop fusion | flops 15197184 | bytes 7559424 | tf_op jit(solution)/shard_map/concatenate | solution.py:41
  238.0 9.0 %fusion.24 = f32[3,8,64,384]{3,2,1,0:T(8,128)S(1)} fusion(f32[3,12,68,388]{3,2,1,0:T(8,128)S(1)} %select_maximum_fusion.12, f32[3,12,66,384]{3,2,1,0:T(8,128)} %get-tuple-element.108, f32[3,12,66,384]{3,2,1,0:T(8,128)} %get-tuple-element.107, f32[3,10,64,384]{3,2,1,0:T(8,128)} %get-tuple-element.129, f32[3,10,64,384]{3,2,1,0:T(8,128)} %get-tuple-element.128, ...), kind=kLoop, calls=%fused_computation.69 | loop fusion | flops 16515072 | bytes 35389440 | tf_op jit(solution)/shard_map/sub | solution.py:81
  257.9 7.9 %all-reduce.22 = (f32[4,384]{1,0:T(4,128)S(1)}, f32[100]{0:T(128)S(1)}) all-reduce(f32[4,384]{1,0:T(4,128)S(1)} %pad_maximum_fusion.14, f32[100]{0:T(128)S(1)} %convolution_bitcast_fusion.4), channel_id=1, replica_groups=mesh['gx_0'=4,'gx_1'=4,'gy_0'=4,'gy_1'=2] {'gx_0'}, use_global_device_ids=true, to_apply=%region_42.43 | all-reduce | flops 1636 | bytes 13088 | tf_op jit(solution)/shard_map/psum | solution.py:22
  265.8 8.9 %all-reduce.18 = (f32[4,384]{1,0:T(4,128)S(1)}, f32[100]{0:T(128)S(1)}) all-reduce(f32[4,384]{1,0:T(4,128)S(1)} %get-tuple-element.61, f32[100]{0:T(128)S(1)} %get-tuple-element.62), channel_id=1, replica_groups=mesh['gx_0'=4,'gx_1'=4,'gy_0'=4,'gy_1'=2] {'gx_1'}, use_global_device_ids=true, to_apply=%region_43.44 | all-reduce | flops 1636 | bytes 13088 | tf_op jit(solution)/shard_map/psum | solution.py:22
  274.7 8.1 %all-reduce.14 = (f32[4,384]{1,0:T(4,128)S(1)}, f32[100]{0:T(128)S(1)}) all-reduce(f32[4,384]{1,0:T(4,128)S(1)} %get-tuple-element.52, f32[100]{0:T(128)S(1)} %get-tuple-element.53), channel_id=1, replica_groups=mesh['gx_0'=4,'gx_1'=4,'gy_0'=4,'gy_1'=2] {'gy_0'}, use_global_device_ids=true, to_apply=%region_44.45 | all-reduce | flops 1636 | bytes 13088 | tf_op jit(solution)/shard_map/psum | solution.py:22
  282.9 6.6 %all-reduce.26 = (f32[4,384]{1,0:T(4,128)S(1)}, f32[100]{0:T(128)S(1)}) all-reduce(f32[4,384]{1,0:T(4,128)S(1)} %get-tuple-element.43, f32[100]{0:T(128)S(1)} %get-tuple-element.44), channel_id=1, replica_groups=mesh['gx_0'=4,'gx_1'=4,'gy_0'=4,'gy_1'=2] {'gy_1'}, use_global_device_ids=true, to_apply=%region_45.46 | all-reduce | flops 1636 | bytes 13088 | tf_op jit(solution)/shard_map/psum | solution.py:22
  310.9 7.7 %select_maximum_fusion.6 = f32[3,12,68,388]{3,2,1,0:T(8,128)S(1)} fusion(f32[3,12,2,384]{3,2,1,0:T(2,128)S(1)} %pad.44, f32[3,12,2,384]{3,2,1,0:T(2,128)S(1)} %pad.45, f32[3,2,64,384]{3,2,1,0:T(8,128)S(1)} %collective-permute-done.8, f32[3,2,64,384]{3,2,1,0:T(8,128)} %collective-permute-done.9, f32[1,8,64,384]{3,2,1,0:T(8,128)S(1)} %copy-done.6, ...), kind=kLoop, calls=%fused_computation.8 | loop fusion | flops 15197184 | bytes 7559424 | tf_op jit(solution)/shard_map/concatenate | solution.py:41
  326.4 8.6 %fusion.15 = f32[3,8,64,384]{3,2,1,0:T(8,128)} fusion(f32[3,12,68,388]{3,2,1,0:T(8,128)S(1)} %select_maximum_fusion.6, f32[3,12,66,384]{3,2,1,0:T(8,128)} %get-tuple-element.106, f32[3,12,66,384]{3,2,1,0:T(8,128)} %get-tuple-element.105, f32[3,10,64,384]{3,2,1,0:T(8,128)} %get-tuple-element.121, f32[3,10,64,384]{3,2,1,0:T(8,128)S(1)} %get-tuple-element.120, ...), kind=kLoop, calls=%fused_computation.57 | loop fusion | flops 16515072 | bytes 35389440 | tf_op jit(solution)/shard_map/sub | solution.py:81
  350.1 14.4 %all-reduce.21 = (f32[4,384]{1,0:T(4,128)S(1)}, f32[100]{0:T(128)S(1)}) all-reduce(f32[4,384]{1,0:T(4,128)S(1)} %pad_maximum_fusion.15, f32[100]{0:T(128)S(1)} %convolution_bitcast_fusion.2), channel_id=1, replica_groups=mesh['gx_0'=4,'gx_1'=4,'gy_0'=4,'gy_1'=2] {'gx_0'}, use_global_device_ids=true, to_apply=%region_58.59 | all-reduce | flops 1636 | bytes 13088 | tf_op jit(solution)/shard_map/psum | solution.py:22
  364.6 7.2 %all-reduce.17 = (f32[4,384]{1,0:T(4,128)S(1)}, f32[100]{0:T(128)S(1)}) all-reduce(f32[4,384]{1,0:T(4,128)S(1)} %get-tuple-element.59, f32[100]{0:T(128)S(1)} %get-tuple-element.60), channel_id=1, replica_groups=mesh['gx_0'=4,'gx_1'=4,'gy_0'=4,'gy_1'=2] {'gx_1'}, use_global_device_ids=true, to_apply=%region_59.60 | all-reduce | flops 1636 | bytes 13088 | tf_op jit(solution)/shard_map/psum | solution.py:22
  371.7 9.7 %all-reduce.13 = (f32[4,384]{1,0:T(4,128)S(1)}, f32[100]{0:T(128)S(1)}) all-reduce(f32[4,384]{1,0:T(4,128)S(1)} %get-tuple-element.50, f32[100]{0:T(128)S(1)} %get-tuple-element.51), channel_id=1, replica_groups=mesh['gx_0'=4,'gx_1'=4,'gy_0'=4,'gy_1'=2] {'gy_0'}, use_global_device_ids=true, to_apply=%region_60.61 | all-reduce | flops 1636 | bytes 13088 | tf_op jit(solution)/shard_map/psum | solution.py:22
  381.4 6.4 %all-reduce.25 = (f32[4,384]{1,0:T(4,128)S(1)}, f32[100]{0:T(128)S(1)}) all-reduce(f32[4,384]{1,0:T(4,128)S(1)} %get-tuple-element.41, f32[100]{0:T(128)S(1)} %get-tuple-element.42), channel_id=1, replica_groups=mesh['gx_0'=4,'gx_1'=4,'gy_0'=4,'gy_1'=2] {'gy_1'}, use_global_device_ids=true, to_apply=%region_61.62 | all-reduce | flops 1636 | bytes 13088 | tf_op jit(solution)/shard_map/psum | solution.py:22
  408.1 7.7 %select_maximum_fusion = f32[3,12,68,388]{3,2,1,0:T(8,128)S(1)} fusion(f32[3,12,2,384]{3,2,1,0:T(2,128)S(1)} %pad.47, f32[3,12,2,384]{3,2,1,0:T(2,128)S(1)} %pad.48, f32[3,2,64,384]{3,2,1,0:T(8,128)S(1)} %collective-permute-done.12, f32[3,2,64,384]{3,2,1,0:T(8,128)} %collective-permute-done.13, f32[1,8,64,384]{3,2,1,0:T(8,128)S(1)} %get-tuple-element.118, ...), kind=kLoop, calls=%fused_computation.2 | loop fusion | flops 15197184 | bytes 7559424 | tf_op jit(solution)/shard_map/concatenate | solution.py:41
  422.1 7.5 %fusion.6 = f32[3,8,64,384]{3,2,1,0:T(8,128)} fusion(f32[3,12,68,388]{3,2,1,0:T(8,128)S(1)} %select_maximum_fusion, f32[3,12,66,384]{3,2,1,0:T(8,128)} %get-tuple-element.104, f32[3,12,66,384]{3,2,1,0:T(8,128)} %get-tuple-element.103, f32[3,10,64,384]{3,2,1,0:T(8,128)S(1)} %get-tuple-element.112, f32[3,10,64,384]{3,2,1,0:T(8,128)S(1)} %get-tuple-element.111, ...), kind=kLoop, calls=%fused_computation.45 | loop fusion | flops 16515072 | bytes 35389440 | tf_op jit(solution)/shard_map/sub | solution.py:81
  (307 shorter events, 161.6 us)
Async XLA Ops:
  1.9 143.1 %collective-permute-start.2 = (f32[3,8,2,384]{3,2,1,0:T(2,128)S(1)}, f32[3,8,2,384]{3,2,1,0:T(2,128)S(1)}, u32[]{:S(2)}, u32[]{:S(2)}) collective-permute-start(f32[3,8,2,384]{3,2,1,0:T(2,128)S(1)} %get-tuple-element.143), channel_id=1, source_target_pairs={{1,0},{2,1},{3,2},{4,3},{5,4},{6,5},{7,6},{0,7},{9,8},{10,9},{11,1... | collective-permute-start | bytes 221192 | tf_op jit(solution)/shard_map/ppermute | solution.py:35
  5.6 139.5 %collective-permute-start.1 = (f32[3,2,64,384]{3,2,1,0:T(8,128)}, f32[3,2,64,384]{3,2,1,0:T(8,128)}, u32[]{:S(2)}, u32[]{:S(2)}) collective-permute-start(f32[3,2,64,384]{3,2,1,0:T(8,128)} %get-tuple-element.145), channel_id=1, source_target_pairs={{0,8},{8,16},{16,24},{24,32},{32,40},{40,48},{48,56},{56,64},{64,7... | collective-permute-start | bytes 1769480 | tf_op jit(solution)/shard_map/ppermute | solution.py:34
  7.4 139.9 %collective-permute-start = (f32[3,2,64,384]{3,2,1,0:T(8,128)}, f32[3,2,64,384]{3,2,1,0:T(8,128)}, u32[]{:S(2)}, u32[]{:S(2)}) collective-permute-start(f32[3,2,64,384]{3,2,1,0:T(8,128)} %get-tuple-element.144), channel_id=1, source_target_pairs={{8,0},{16,8},{24,16},{32,24},{40,32},{48,40},{56,48},{64,56},{72,6... | collective-permute-start | bytes 1769480 | tf_op jit(solution)/shard_map/ppermute | solution.py:35
  12.0 133.1 %collective-permute-start.3 = (f32[3,8,2,384]{3,2,1,0:T(2,128)S(1)}, f32[3,8,2,384]{3,2,1,0:T(2,128)S(1)}, u32[]{:S(2)}, u32[]{:S(2)}) collective-permute-start(f32[3,8,2,384]{3,2,1,0:T(2,128)S(1)} %get-tuple-element.142), channel_id=1, source_target_pairs={{0,1},{1,2},{2,3},{3,4},{4,5},{5,6},{6,7},{7,0},{8,9},{9,10},{10,1... | collective-permute-start | bytes 221192 | tf_op jit(solution)/shard_map/ppermute | solution.py:34
  14.9 121.3 %copy-start.53 = (s32[100]{0:T(128)S(1)}, s32[100]{0:T(128)}, u32[]{:S(2)}) copy-start(s32[100]{0:T(128)} %param.13) | copy-start | bytes 1204
  14.9 121.5 %copy-start.41 = (s32[100]{0:T(128)S(1)}, s32[100]{0:T(128)}, u32[]{:S(2)}) copy-start(s32[100]{0:T(128)} %param.14) | copy-start | bytes 1204
  163.2 74.8 %copy-start.1 = (f32[8,64,384]{2,1,0:T(8,128)}, f32[8,64,384]{2,1,0:T(8,128)S(1)}, u32[]{:S(2)}) copy-start(f32[8,64,384]{2,1,0:T(8,128)S(1)} %get-tuple-element.99) | copy-start | bytes 2359300
  197.8 22.3 %collective-permute-start.6 = (f32[3,8,2,384]{3,2,1,0:T(2,128)S(1)}, f32[3,8,2,384]{3,2,1,0:T(2,128)S(1)}, u32[]{:S(2)}, u32[]{:S(2)}) collective-permute-start(f32[3,8,2,384]{3,2,1,0:T(2,128)S(1)} %get-tuple-element.133), channel_id=1, source_target_pairs={{1,0},{2,1},{3,2},{4,3},{5,4},{6,5},{7,6},{0,7},{9,8},{10,9},{11,1... | collective-permute-start | bytes 221192 | tf_op jit(solution)/shard_map/ppermute | solution.py:35
  198.1 22.0 %collective-permute-start.7 = (f32[3,8,2,384]{3,2,1,0:T(2,128)S(1)}, f32[3,8,2,384]{3,2,1,0:T(2,128)S(1)}, u32[]{:S(2)}, u32[]{:S(2)}) collective-permute-start(f32[3,8,2,384]{3,2,1,0:T(2,128)S(1)} %get-tuple-element.132), channel_id=1, source_target_pairs={{0,1},{1,2},{2,3},{3,4},{4,5},{5,6},{6,7},{7,0},{8,9},{9,10},{10,1... | collective-permute-start | bytes 221192 | tf_op jit(solution)/shard_map/ppermute | solution.py:34
  199.6 20.5 %collective-permute-start.4 = (f32[3,2,64,384]{3,2,1,0:T(8,128)}, f32[3,2,64,384]{3,2,1,0:T(8,128)}, u32[]{:S(2)}, u32[]{:S(2)}) collective-permute-start(f32[3,2,64,384]{3,2,1,0:T(8,128)} %get-tuple-element.131), channel_id=1, source_target_pairs={{8,0},{16,8},{24,16},{32,24},{40,32},{48,40},{56,48},{64,56},{72,6... | collective-permute-start | bytes 1769480 | tf_op jit(solution)/shard_map/ppermute | solution.py:35
  200.6 19.5 %collective-permute-start.5 = (f32[3,2,64,384]{3,2,1,0:T(8,128)}, f32[3,2,64,384]{3,2,1,0:T(8,128)}, u32[]{:S(2)}, u32[]{:S(2)}) collective-permute-start(f32[3,2,64,384]{3,2,1,0:T(8,128)} %get-tuple-element.130), channel_id=1, source_target_pairs={{0,8},{8,16},{16,24},{24,32},{32,40},{40,48},{48,56},{56,64},{64,7... | collective-permute-start | bytes 1769480 | tf_op jit(solution)/shard_map/ppermute | solution.py:34
  289.5 21.3 %collective-permute-start.10 = (f32[3,8,2,384]{3,2,1,0:T(2,128)S(1)}, f32[3,8,2,384]{3,2,1,0:T(2,128)S(1)}, u32[]{:S(2)}, u32[]{:S(2)}) collective-permute-start(f32[3,8,2,384]{3,2,1,0:T(2,128)S(1)} %get-tuple-element.125), channel_id=1, source_target_pairs={{1,0},{2,1},{3,2},{4,3},{5,4},{6,5},{7,6},{0,7},{9,8},{10,9},{11,1... | collective-permute-start | bytes 221192 | tf_op jit(solution)/shard_map/ppermute | solution.py:35
  289.8 21.0 %collective-permute-start.11 = (f32[3,8,2,384]{3,2,1,0:T(2,128)S(1)}, f32[3,8,2,384]{3,2,1,0:T(2,128)S(1)}, u32[]{:S(2)}, u32[]{:S(2)}) collective-permute-start(f32[3,8,2,384]{3,2,1,0:T(2,128)S(1)} %get-tuple-element.124), channel_id=1, source_target_pairs={{0,1},{1,2},{2,3},{3,4},{4,5},{5,6},{6,7},{7,0},{8,9},{9,10},{10,1... | collective-permute-start | bytes 221192 | tf_op jit(solution)/shard_map/ppermute | solution.py:34
  291.2 19.7 %collective-permute-start.8 = (f32[3,2,64,384]{3,2,1,0:T(8,128)}, f32[3,2,64,384]{3,2,1,0:T(8,128)S(1)}, u32[]{:S(2)}, u32[]{:S(2)}) collective-permute-start(f32[3,2,64,384]{3,2,1,0:T(8,128)} %get-tuple-element.123), channel_id=1, source_target_pairs={{8,0},{16,8},{24,16},{32,24},{40,32},{48,40},{56,48},{64,56},{72,6... | collective-permute-start | bytes 1769480 | tf_op jit(solution)/shard_map/ppermute | solution.py:35
  291.2 19.7 %collective-permute-start.9 = (f32[3,2,64,384]{3,2,1,0:T(8,128)}, f32[3,2,64,384]{3,2,1,0:T(8,128)}, u32[]{:S(2)}, u32[]{:S(2)}) collective-permute-start(f32[3,2,64,384]{3,2,1,0:T(8,128)} %get-tuple-element.122), channel_id=1, source_target_pairs={{0,8},{8,16},{16,24},{24,32},{32,40},{40,48},{48,56},{56,64},{64,7... | collective-permute-start | bytes 1769480 | tf_op jit(solution)/shard_map/ppermute | solution.py:34
  340.3 65.5 %copy-start.58 = (f32[1,4]{1,0:T(1,128)S(1)}, f32[1,4]{1,0:T(1,128)}, u32[]{:S(2)}) copy-start(f32[1,4]{1,0:T(1,128)} %param.15) | copy-start | bytes 52
  340.3 65.5 %copy-start.60 = (s32[100]{0:T(128)S(1)}, s32[100]{0:T(128)}, u32[]{:S(2)}) copy-start(s32[100]{0:T(128)} %copy-done.59) | copy-start | bytes 1204
  340.4 67.0 %copy-start.33 = (f32[4,384]{1,0:T(4,128)S(1)}, f32[4,384]{1,0:T(4,128)}, u32[]{:S(2)}) copy-start(f32[4,384]{1,0:T(4,128)} %copy-done.32) | copy-start | bytes 18436
  340.4 67.0 %copy-start.39 = (f32[1,384]{1,0:T(1,128)S(1)}, f32[1,384]{1,0:T(1,128)}, u32[]{:S(2)}) copy-start(f32[1,384]{1,0:T(1,128)} %fusion.105) | copy-start | bytes 4612
  340.4 67.0 %copy-start.40 = (f32[1,384]{1,0:T(1,128)S(1)}, f32[1,384]{1,0:T(1,128)}, u32[]{:S(2)}) copy-start(f32[1,384]{1,0:T(1,128)} %fusion.104) | copy-start | bytes 4612
  342.3 65.7 %collective-permute-start.14 = (f32[3,8,2,384]{3,2,1,0:T(2,128)S(1)}, f32[3,8,2,384]{3,2,1,0:T(2,128)S(1)}, u32[]{:S(2)}, u32[]{:S(2)}) collective-permute-start(f32[3,8,2,384]{3,2,1,0:T(2,128)S(1)} %get-tuple-element.116), channel_id=1, source_target_pairs={{1,0},{2,1},{3,2},{4,3},{5,4},{6,5},{7,6},{0,7},{9,8},{10,9},{11,1... | collective-permute-start | bytes 221192 | tf_op jit(solution)/shard_map/ppermute | solution.py:35
  342.4 65.6 %collective-permute-start.15 = (f32[3,8,2,384]{3,2,1,0:T(2,128)S(1)}, f32[3,8,2,384]{3,2,1,0:T(2,128)S(1)}, u32[]{:S(2)}, u32[]{:S(2)}) collective-permute-start(f32[3,8,2,384]{3,2,1,0:T(2,128)S(1)} %get-tuple-element.115), channel_id=1, source_target_pairs={{0,1},{1,2},{2,3},{3,4},{4,5},{5,6},{6,7},{7,0},{8,9},{9,10},{10,1... | collective-permute-start | bytes 221192 | tf_op jit(solution)/shard_map/ppermute | solution.py:34
  344.0 64.1 %collective-permute-start.12 = (f32[3,2,64,384]{3,2,1,0:T(8,128)}, f32[3,2,64,384]{3,2,1,0:T(8,128)S(1)}, u32[]{:S(2)}, u32[]{:S(2)}) collective-permute-start(f32[3,2,64,384]{3,2,1,0:T(8,128)} %get-tuple-element.114), channel_id=1, source_target_pairs={{8,0},{16,8},{24,16},{32,24},{40,32},{48,40},{56,48},{64,56},{72,6... | collective-permute-start | bytes 1769480 | tf_op jit(solution)/shard_map/ppermute | solution.py:35
  347.3 60.8 %collective-permute-start.13 = (f32[3,2,64,384]{3,2,1,0:T(8,128)}, f32[3,2,64,384]{3,2,1,0:T(8,128)}, u32[]{:S(2)}, u32[]{:S(2)}) collective-permute-start(f32[3,2,64,384]{3,2,1,0:T(8,128)} %get-tuple-element.113), channel_id=1, source_target_pairs={{0,8},{8,16},{16,24},{24,32},{32,40},{40,48},{48,56},{56,64},{64,7... | collective-permute-start | bytes 1769480 | tf_op jit(solution)/shard_map/ppermute | solution.py:34
  (56 other events, 1017.5 us)
where the time goes:
time: 441 us; the launch traced here: 434 us
  blocking collectives  192 us (44%)
  other arithmetic  126 us (29%)
  local copies, waits for them, and re-layouts  57.6 us (13%)
  between operations  24.7 us (6%)
  starting transfers between devices  21.4 us (5%)
  matrix products  12.6 us (3%)
    psum x16, blocking collectives, by_axis(): shard = lax.psum(shard, axis)  129 us
    all_gather x1, blocking collectives, local(): state_all = lax.all_gather(controller_state[0], GX_GY, axis=0, tiled=True)  62.9 us
    concatenate x10, other arithmetic, padded_2(): jnp.concatenate([jnp.pad(low, around), shard, jnp.pad(high, around)], axi...  49.4 us
    dynamic_update_slice x16, local copies, waits for them, and re-layouts, local(): lax.dynamic_update_slice(force_field, previous - slot_factor[slot_index]...  36.7 us
    sub x4, other arithmetic, tendency(): return VISCOSITY * laplacian - advection  33.3 us
    sub x16, other arithmetic, local(): previous - slot_factor[slot_index] * weights_local[slot_index][None]  17.7 us
    ppermute x8, starting transfers between devices, padded_2(): lax.ppermute(first, axis, [(b, a) for a, b in up])  11.1 us
    dot_general x4, matrix products, local(): numerator_part = jnp.dot(contribution, slot_onehot, precision=HIGHEST)  10.8 us
  transfers between devices with their start and end apart: 16, of which 0 were waited for; matrix products, arithmetic and copies ran while one was open for 18% of the time, Pallas kernels for 0%

commit v1 on v0

--- a/solution.py
+++ b/solution.py
@@ -19,7 +19,7 @@
 
 def by_axis(shard, axes):
     for axis in axes:
-        shard = lax.psum(shard, axis)
+        shard = jnp.sum(lax.all_gather(shard, axis), axis=0)
     return shard
 
 

time: 441 us -> 620 us (1.41)
  blocking collectives: 192 us -> 358 us
  local copies, waits for them, and re-layouts: 57.6 us -> 67.2 us
    all_gather x0 -> x16, blocking collectives: none -> 161 us  [by_axis(): shard = jnp.sum(lax.all_gather(shard, axis), axis=0)]
    unnamed x0 -> x16, blocking collectives: none -> 133 us
    psum x16 -> x0, blocking collectives: 129 us -> none  [by_axis(): shard = lax.psum(shard, axis)]
    unnamed x132 -> x190, local copies, waits for them, and re-layouts: 5.62 us -> 12.9 us
  transfers between devices with their start and end apart: 16 -> 16, of which waited for: 0 -> 0; matrix products, arithmetic and copies ran while one was open for 18% -> 15% of each run, Pallas kernels for 0% -> 0%
where the time goes in v1:
time: 620 us; the launch traced here: 612 us
  blocking collectives  358 us (58%)
  other arithmetic  127 us (20%)
  local copies, waits for them, and re-layouts  67.2 us (11%)
  between operations  27.3 us (4%)
  starting transfers between devices  19.7 us (3%)
  matrix products  12.5 us (2%)
    all_gather x16, blocking collectives, by_axis(): shard = jnp.sum(lax.all_gather(shard, axis), axis=0)  161 us
    unnamed x16, blocking collectives  133 us
    all_gather x1, blocking collectives, local(): state_all = lax.all_gather(controller_state[0], GX_GY, axis=0, tiled=True)  63.1 us
    concatenate x10, other arithmetic, padded_2(): jnp.concatenate([jnp.pad(low, around), shard, jnp.pad(high, around)], axi...  49.4 us
    dynamic_update_slice x16, local copies, waits for them, and re-layouts, local(): lax.dynamic_update_slice(force_field, previous - slot_factor[slot_index]...  36.5 us
    sub x4, other arithmetic, tendency(): return VISCOSITY * laplacian - advection  33.3 us
    sub x16, other arithmetic, local(): previous - slot_factor[slot_index] * weights_local[slot_index][None]  17.6 us
    unnamed x190, local copies, waits for them, and re-layouts  12.9 us
  transfers between devices with their start and end apart: 16, of which 0 were waited for; matrix products, arithmetic and copies ran while one was open for 15% of the time, Pallas kernels for 0%

profile of v1, /device:TPU:1, one launch (start us, length us, event | category | flops | bytes accessed | tf_op | source)
XLA Modules:
  0.0 611.5 jit_solution(14992730794082423227)
XLA Ops:
  31.2 9.1 %all-gather.37 = f32[4,4,384]{2,1,0:T(4,128)S(1)} all-gather(f32[1,4,384]{2,1,0:T(4,128)S(1)} %maximum_bitcast_fusion), channel_id=2, replica_groups=mesh['gx_0'=4,'gx_1'=4,'gy_0'=4,'gy_1'=2] {'gx_0'}, dimensions={0}, use_global_device_ids=true | all-gather | bytes 30720 | tf_op jit(solution)/shard_map/all_gather | solution.py:22
  40.3 9.1 %all-gather.38 = f32[4,4,384]{2,1,0:T(4,128)S(1)} all-gather(f32[1,4,384]{2,1,0:T(4,128)S(1)} %bitcast.406), channel_id=3, replica_groups=mesh['gx_0'=4,'gx_1'=4,'gy_0'=4,'gy_1'=2] {'gx_1'}, dimensions={0}, use_global_device_ids=true | all-gather | bytes 30720 | tf_op jit(solution)/shard_map/all_gather | solution.py:22
  49.4 10.0 %all-gather.39 = f32[4,4,384]{2,1,0:T(4,128)S(1)} all-gather(f32[1,4,384]{2,1,0:T(4,128)S(1)} %bitcast.407), channel_id=4, replica_groups=mesh['gx_0'=4,'gx_1'=4,'gy_0'=4,'gy_1'=2] {'gy_0'}, dimensions={0}, use_global_device_ids=true | all-gather | bytes 30720 | tf_op jit(solution)/shard_map/all_gather | solution.py:22
  59.5 10.2 %all-gather.40 = f32[2,4,384]{2,1,0:T(4,128)S(1)} all-gather(f32[1,4,384]{2,1,0:T(4,128)S(1)} %bitcast.402), channel_id=5, replica_groups=mesh['gx_0'=4,'gx_1'=4,'gy_0'=4,'gy_1'=2] {'gy_1'}, dimensions={0}, use_global_device_ids=true | all-gather | bytes 18432 | tf_op jit(solution)/shard_map/all_gather | solution.py:22
  109.5 8.5 %all-reduce.36 = (f32[200]{0:T(256)S(1)}, f32[200]{0:T(256)S(1)}) all-reduce(f32[200]{0:T(256)S(1)} %dynamic-update-slice.3, f32[200]{0:T(256)S(1)} %dynamic-update-slice.7), channel_id=9, replica_groups=mesh['gx_0'=4,'gx_1'=4,'gy_0'=4,'gy_1'=2] {'gy_1'}, use_global_device_ids=true, to_apply=%add.15 | all-reduce | flops 400 | bytes 3200
  118.2 63.1 %all-reduce.20 = f32[512]{0:T(512)S(1)} all-reduce(f32[512]{0:T(512)S(1)} %bitcast_dynamic-update-slice_fusion), channel_id=14, replica_groups=mesh['gx_0'=4,'gx_1'=4,'gy_0'=4,'gy_1'=2] {'gx_0','gx_1','gy_0','gy_1'}, use_global_device_ids=true, to_apply=%add.20 | all-reduce | flops 512 | bytes 4096 | tf_op jit(solution)/shard_map/all_gather | solution.py:152
  211.4 9.1 %all-gather.41 = f32[4,4,384]{2,1,0:T(4,128)S(1)} all-gather(f32[1,4,384]{2,1,0:T(4,128)S(1)} %maximum_bitcast_fusion.1), channel_id=15, replica_groups=mesh['gx_0'=4,'gx_1'=4,'gy_0'=4,'gy_1'=2] {'gx_0'}, dimensions={0}, use_global_device_ids=true | all-gather | bytes 30720 | tf_op jit(solution)/shard_map/all_gather | solution.py:22
  220.5 9.1 %all-gather.42 = f32[4,4,384]{2,1,0:T(4,128)S(1)} all-gather(f32[1,4,384]{2,1,0:T(4,128)S(1)} %bitcast.408), channel_id=16, replica_groups=mesh['gx_0'=4,'gx_1'=4,'gy_0'=4,'gy_1'=2] {'gx_1'}, dimensions={0}, use_global_device_ids=true | all-gather | bytes 30720 | tf_op jit(solution)/shard_map/all_gather | solution.py:22
  229.6 9.1 %all-gather.43 = f32[4,4,384]{2,1,0:T(4,128)S(1)} all-gather(f32[1,4,384]{2,1,0:T(4,128)S(1)} %bitcast.409), channel_id=17, replica_groups=mesh['gx_0'=4,'gx_1'=4,'gy_0'=4,'gy_1'=2] {'gy_0'}, dimensions={0}, use_global_device_ids=true | all-gather | bytes 30720 | tf_op jit(solution)/shard_map/all_gather | solution.py:22
  238.7 10.9 %all-gather.44 = f32[2,4,384]{2,1,0:T(4,128)S(1)} all-gather(f32[1,4,384]{2,1,0:T(4,128)S(1)} %bitcast.403), channel_id=18, replica_groups=mesh['gx_0'=4,'gx_1'=4,'gy_0'=4,'gy_1'=2] {'gy_1'}, dimensions={0}, use_global_device_ids=true | all-gather | bytes 18432 | tf_op jit(solution)/shard_map/all_gather | solution.py:22
  256.5 15.2 %all-reduce.21 = f32[400]{0:T(512)S(1)} all-reduce(f32[400]{0:T(512)S(1)} %dynamic-update-slice.9), channel_id=19, replica_groups=mesh['gx_0'=4,'gx_1'=4,'gy_0'=4,'gy_1'=2] {'gx_0'}, use_global_device_ids=true, to_apply=%add.21 | all-reduce | flops 400 | bytes 3200
  331.1 9.0 %fusion.24 = f32[3,8,64,384]{3,2,1,0:T(8,128)S(1)} fusion(f32[3,12,68,388]{3,2,1,0:T(8,128)S(1)} %select_maximum_fusion.12, f32[3,12,66,384]{3,2,1,0:T(8,128)} %get-tuple-element.80, f32[3,12,66,384]{3,2,1,0:T(8,128)} %get-tuple-element.79, f32[3,10,64,384]{3,2,1,0:T(8,128)} %get-tuple-element.101, f32[3,10,64,384]{3,2,1,0:T(8,128)} %get-tuple-element.100, ...), kind=kLoop, calls=%fused_computation.69 | loop fusion | flops 16515072 | bytes 35389440 | tf_op jit(solution)/shard_map/sub | solution.py:81
  348.4 9.3 %all-gather.45 = f32[4,4,384]{2,1,0:T(4,128)S(1)} all-gather(f32[1,4,384]{2,1,0:T(4,128)S(1)} %maximum_bitcast_fusion.2), channel_id=23, replica_groups=mesh['gx_0'=4,'gx_1'=4,'gy_0'=4,'gy_1'=2] {'gx_0'}, dimensions={0}, use_global_device_ids=true | all-gather | bytes 30720 | tf_op jit(solution)/shard_map/all_gather | solution.py:22
  357.8 9.1 %all-gather.46 = f32[4,4,384]{2,1,0:T(4,128)S(1)} all-gather(f32[1,4,384]{2,1,0:T(4,128)S(1)} %bitcast.410), channel_id=24, replica_groups=mesh['gx_0'=4,'gx_1'=4,'gy_0'=4,'gy_1'=2] {'gx_1'}, dimensions={0}, use_global_device_ids=true | all-gather | bytes 30720 | tf_op jit(solution)/shard_map/all_gather | solution.py:22
  366.8 9.1 %all-gather.47 = f32[4,4,384]{2,1,0:T(4,128)S(1)} all-gather(f32[1,4,384]{2,1,0:T(4,128)S(1)} %bitcast.411), channel_id=25, replica_groups=mesh['gx_0'=4,'gx_1'=4,'gy_0'=4,'gy_1'=2] {'gy_0'}, dimensions={0}, use_global_device_ids=true | all-gather | bytes 30720 | tf_op jit(solution)/shard_map/all_gather | solution.py:22
  375.9 10.2 %all-gather.48 = f32[2,4,384]{2,1,0:T(4,128)S(1)} all-gather(f32[1,4,384]{2,1,0:T(4,128)S(1)} %bitcast.404), channel_id=26, replica_groups=mesh['gx_0'=4,'gx_1'=4,'gy_0'=4,'gy_1'=2] {'gy_1'}, dimensions={0}, use_global_device_ids=true | all-gather | bytes 18432 | tf_op jit(solution)/shard_map/all_gather | solution.py:22
  392.3 15.2 %all-reduce.25 = f32[400]{0:T(512)S(1)} all-reduce(f32[400]{0:T(512)S(1)} %dynamic-update-slice.13), channel_id=27, replica_groups=mesh['gx_0'=4,'gx_1'=4,'gy_0'=4,'gy_1'=2] {'gx_0'}, use_global_device_ids=true, to_apply=%add.25 | all-reduce | flops 400 | bytes 3200
  463.5 8.6 %fusion.15 = f32[3,8,64,384]{3,2,1,0:T(8,128)} fusion(f32[3,12,68,388]{3,2,1,0:T(8,128)S(1)} %select_maximum_fusion.6, f32[3,12,66,384]{3,2,1,0:T(8,128)} %get-tuple-element.78, f32[3,12,66,384]{3,2,1,0:T(8,128)} %get-tuple-element.77, f32[3,10,64,384]{3,2,1,0:T(8,128)} %get-tuple-element.93, f32[3,10,64,384]{3,2,1,0:T(8,128)S(1)} %get-tuple-element.92, ...), kind=kLoop, calls=%fused_computation.57 | loop fusion | flops 16515072 | bytes 35389440 | tf_op jit(solution)/shard_map/sub | solution.py:81
  482.6 19.2 %all-gather.49 = f32[4,4,384]{2,1,0:T(4,128)S(1)} all-gather(f32[1,4,384]{2,1,0:T(4,128)S(1)} %maximum_bitcast_fusion.3), channel_id=31, replica_groups=mesh['gx_0'=4,'gx_1'=4,'gy_0'=4,'gy_1'=2] {'gx_0'}, dimensions={0}, use_global_device_ids=true | all-gather | bytes 30720 | tf_op jit(solution)/shard_map/all_gather | solution.py:22
  501.8 9.1 %all-gather.50 = f32[4,4,384]{2,1,0:T(4,128)S(1)} all-gather(f32[1,4,384]{2,1,0:T(4,128)S(1)} %bitcast.412), channel_id=32, replica_groups=mesh['gx_0'=4,'gx_1'=4,'gy_0'=4,'gy_1'=2] {'gx_1'}, dimensions={0}, use_global_device_ids=true | all-gather | bytes 30720 | tf_op jit(solution)/shard_map/all_gather | solution.py:22
  510.9 9.1 %all-gather.51 = f32[4,4,384]{2,1,0:T(4,128)S(1)} all-gather(f32[1,4,384]{2,1,0:T(4,128)S(1)} %bitcast.413), channel_id=33, replica_groups=mesh['gx_0'=4,'gx_1'=4,'gy_0'=4,'gy_1'=2] {'gy_0'}, dimensions={0}, use_global_device_ids=true | all-gather | bytes 30720 | tf_op jit(solution)/shard_map/all_gather | solution.py:22
  519.9 9.8 %all-gather.52 = f32[2,4,384]{2,1,0:T(4,128)S(1)} all-gather(f32[1,4,384]{2,1,0:T(4,128)S(1)} %bitcast.405), channel_id=34, replica_groups=mesh['gx_0'=4,'gx_1'=4,'gy_0'=4,'gy_1'=2] {'gy_1'}, dimensions={0}, use_global_device_ids=true | all-gather | bytes 18432 | tf_op jit(solution)/shard_map/all_gather | solution.py:22
  539.9 8.9 %all-reduce.30 = f32[400]{0:T(512)S(1)} all-reduce(f32[400]{0:T(512)S(1)} %dynamic-update-slice.18), channel_id=36, replica_groups=mesh['gx_0'=4,'gx_1'=4,'gy_0'=4,'gy_1'=2] {'gx_1'}, use_global_device_ids=true, to_apply=%add.30 | all-reduce | flops 400 | bytes 3200
  556.0 8.8 %all-reduce.32 = f32[200]{0:T(256)S(1)} all-reduce(f32[200]{0:T(256)S(1)} %dynamic-update-slice.20), channel_id=38, replica_groups=mesh['gx_0'=4,'gx_1'=4,'gy_0'=4,'gy_1'=2] {'gy_1'}, use_global_device_ids=true, to_apply=%add.32 | all-reduce | flops 200 | bytes 1600
  (436 shorter events, 285.6 us)
Async XLA Ops:
  1.9 189.1 %collective-permute-start.2 = (f32[3,8,2,384]{3,2,1,0:T(2,128)S(1)}, f32[3,8,2,384]{3,2,1,0:T(2,128)S(1)}, u32[]{:S(2)}, u32[]{:S(2)}) collective-permute-start(f32[3,8,2,384]{3,2,1,0:T(2,128)S(1)} %get-tuple-element.115), channel_id=1, source_target_pairs={{1,0},{2,1},{3,2},{4,3},{5,4},{6,5},{7,6},{0,7},{9,8},{10,9},{11,1... | collective-permute-start | bytes 221192 | tf_op jit(solution)/shard_map/ppermute | solution.py:35
  5.6 185.5 %collective-permute-start.1 = (f32[3,2,64,384]{3,2,1,0:T(8,128)}, f32[3,2,64,384]{3,2,1,0:T(8,128)}, u32[]{:S(2)}, u32[]{:S(2)}) collective-permute-start(f32[3,2,64,384]{3,2,1,0:T(8,128)} %get-tuple-element.117), channel_id=1, source_target_pairs={{0,8},{8,16},{16,24},{24,32},{32,40},{40,48},{48,56},{56,64},{64,7... | collective-permute-start | bytes 1769480 | tf_op jit(solution)/shard_map/ppermute | solution.py:34
  7.4 185.9 %collective-permute-start = (f32[3,2,64,384]{3,2,1,0:T(8,128)}, f32[3,2,64,384]{3,2,1,0:T(8,128)}, u32[]{:S(2)}, u32[]{:S(2)}) collective-permute-start(f32[3,2,64,384]{3,2,1,0:T(8,128)} %get-tuple-element.116), channel_id=1, source_target_pairs={{8,0},{16,8},{24,16},{32,24},{40,32},{48,40},{56,48},{64,56},{72,6... | collective-permute-start | bytes 1769480 | tf_op jit(solution)/shard_map/ppermute | solution.py:35
  12.0 179.1 %collective-permute-start.3 = (f32[3,8,2,384]{3,2,1,0:T(2,128)S(1)}, f32[3,8,2,384]{3,2,1,0:T(2,128)S(1)}, u32[]{:S(2)}, u32[]{:S(2)}) collective-permute-start(f32[3,8,2,384]{3,2,1,0:T(2,128)S(1)} %get-tuple-element.114), channel_id=1, source_target_pairs={{0,1},{1,2},{2,3},{3,4},{4,5},{5,6},{6,7},{7,0},{8,9},{9,10},{10,1... | collective-permute-start | bytes 221192 | tf_op jit(solution)/shard_map/ppermute | solution.py:34
  14.9 166.4 %copy-start.56 = (s32[100]{0:T(128)S(1)}, s32[100]{0:T(128)}, u32[]{:S(2)}) copy-start(s32[100]{0:T(128)} %param.13) | copy-start | bytes 1204
  14.9 167.1 %copy-start.47 = (s32[100]{0:T(128)S(1)}, s32[100]{0:T(128)}, u32[]{:S(2)}) copy-start(s32[100]{0:T(128)} %param.14) | copy-start | bytes 1204
  209.2 121.9 %copy-start.1 = (f32[8,64,384]{2,1,0:T(8,128)}, f32[8,64,384]{2,1,0:T(8,128)S(1)}, u32[]{:S(2)}) copy-start(f32[8,64,384]{2,1,0:T(8,128)S(1)} %get-tuple-element.71) | copy-start | bytes 2359300
  249.6 63.6 %collective-permute-start.6 = (f32[3,8,2,384]{3,2,1,0:T(2,128)S(1)}, f32[3,8,2,384]{3,2,1,0:T(2,128)S(1)}, u32[]{:S(2)}, u32[]{:S(2)}) collective-permute-start(f32[3,8,2,384]{3,2,1,0:T(2,128)S(1)} %get-tuple-element.105), channel_id=1, source_target_pairs={{1,0},{2,1},{3,2},{4,3},{5,4},{6,5},{7,6},{0,7},{9,8},{10,9},{11,1... | collective-permute-start | bytes 221192 | tf_op jit(solution)/shard_map/ppermute | solution.py:35
  250.0 63.2 %collective-permute-start.7 = (f32[3,8,2,384]{3,2,1,0:T(2,128)S(1)}, f32[3,8,2,384]{3,2,1,0:T(2,128)S(1)}, u32[]{:S(2)}, u32[]{:S(2)}) collective-permute-start(f32[3,8,2,384]{3,2,1,0:T(2,128)S(1)} %get-tuple-element.104), channel_id=1, source_target_pairs={{0,1},{1,2},{2,3},{3,4},{4,5},{5,6},{6,7},{7,0},{8,9},{9,10},{10,1... | collective-permute-start | bytes 221192 | tf_op jit(solution)/shard_map/ppermute | solution.py:34
  251.4 61.9 %collective-permute-start.4 = (f32[3,2,64,384]{3,2,1,0:T(8,128)}, f32[3,2,64,384]{3,2,1,0:T(8,128)}, u32[]{:S(2)}, u32[]{:S(2)}) collective-permute-start(f32[3,2,64,384]{3,2,1,0:T(8,128)} %get-tuple-element.103), channel_id=1, source_target_pairs={{8,0},{16,8},{24,16},{32,24},{40,32},{48,40},{56,48},{64,56},{72,6... | collective-permute-start | bytes 1769480 | tf_op jit(solution)/shard_map/ppermute | solution.py:35
  253.7 59.6 %collective-permute-start.5 = (f32[3,2,64,384]{3,2,1,0:T(8,128)}, f32[3,2,64,384]{3,2,1,0:T(8,128)}, u32[]{:S(2)}, u32[]{:S(2)}) collective-permute-start(f32[3,2,64,384]{3,2,1,0:T(8,128)} %get-tuple-element.102), channel_id=1, source_target_pairs={{0,8},{8,16},{16,24},{24,32},{32,40},{40,48},{48,56},{56,64},{64,7... | collective-permute-start | bytes 1769480 | tf_op jit(solution)/shard_map/ppermute | solution.py:34
  386.2 61.7 %collective-permute-start.10 = (f32[3,8,2,384]{3,2,1,0:T(2,128)S(1)}, f32[3,8,2,384]{3,2,1,0:T(2,128)S(1)}, u32[]{:S(2)}, u32[]{:S(2)}) collective-permute-start(f32[3,8,2,384]{3,2,1,0:T(2,128)S(1)} %get-tuple-element.97), channel_id=1, source_target_pairs={{1,0},{2,1},{3,2},{4,3},{5,4},{6,5},{7,6},{0,7},{9,8},{10,9},{11,1... | collective-permute-start | bytes 221192 | tf_op jit(solution)/shard_map/ppermute | solution.py:35
  386.5 61.4 %collective-permute-start.11 = (f32[3,8,2,384]{3,2,1,0:T(2,128)S(1)}, f32[3,8,2,384]{3,2,1,0:T(2,128)S(1)}, u32[]{:S(2)}, u32[]{:S(2)}) collective-permute-start(f32[3,8,2,384]{3,2,1,0:T(2,128)S(1)} %get-tuple-element.96), channel_id=1, source_target_pairs={{0,1},{1,2},{2,3},{3,4},{4,5},{5,6},{6,7},{7,0},{8,9},{9,10},{10,1... | collective-permute-start | bytes 221192 | tf_op jit(solution)/shard_map/ppermute | solution.py:34
  387.9 60.0 %collective-permute-start.8 = (f32[3,2,64,384]{3,2,1,0:T(8,128)}, f32[3,2,64,384]{3,2,1,0:T(8,128)S(1)}, u32[]{:S(2)}, u32[]{:S(2)}) collective-permute-start(f32[3,2,64,384]{3,2,1,0:T(8,128)} %get-tuple-element.95), channel_id=1, source_target_pairs={{8,0},{16,8},{24,16},{32,24},{40,32},{48,40},{56,48},{64,56},{72,6... | collective-permute-start | bytes 1769480 | tf_op jit(solution)/shard_map/ppermute | solution.py:35
  389.5 58.5 %collective-permute-start.9 = (f32[3,2,64,384]{3,2,1,0:T(8,128)}, f32[3,2,64,384]{3,2,1,0:T(8,128)}, u32[]{:S(2)}, u32[]{:S(2)}) collective-permute-start(f32[3,2,64,384]{3,2,1,0:T(8,128)} %get-tuple-element.94), channel_id=1, source_target_pairs={{0,8},{8,16},{16,24},{24,32},{32,40},{40,48},{48,56},{56,64},{64,7... | collective-permute-start | bytes 1769480 | tf_op jit(solution)/shard_map/ppermute | solution.py:34
  477.4 105.4 %copy-start.61 = (f32[1,4]{1,0:T(1,128)S(1)}, f32[1,4]{1,0:T(1,128)}, u32[]{:S(2)}) copy-start(f32[1,4]{1,0:T(1,128)} %param.15) | copy-start | bytes 52
  477.4 105.4 %copy-start.63 = (s32[100]{0:T(128)S(1)}, s32[100]{0:T(128)}, u32[]{:S(2)}) copy-start(s32[100]{0:T(128)} %copy-done.62) | copy-start | bytes 1204
  477.5 106.9 %copy-start.33 = (f32[4,384]{1,0:T(4,128)S(1)}, f32[4,384]{1,0:T(4,128)}, u32[]{:S(2)}) copy-start(f32[4,384]{1,0:T(4,128)} %copy-done.32) | copy-start | bytes 18436
  477.5 106.9 %copy-start.42 = (f32[1,384]{1,0:T(1,128)S(1)}, f32[1,384]{1,0:T(1,128)}, u32[]{:S(2)}) copy-start(f32[1,384]{1,0:T(1,128)} %fusion.105) | copy-start | bytes 4612
  477.5 106.9 %copy-start.43 = (f32[1,384]{1,0:T(1,128)S(1)}, f32[1,384]{1,0:T(1,128)}, u32[]{:S(2)}) copy-start(f32[1,384]{1,0:T(1,128)} %fusion.104) | copy-start | bytes 4612
  479.3 105.7 %collective-permute-start.14 = (f32[3,8,2,384]{3,2,1,0:T(2,128)S(1)}, f32[3,8,2,384]{3,2,1,0:T(2,128)S(1)}, u32[]{:S(2)}, u32[]{:S(2)}) collective-permute-start(f32[3,8,2,384]{3,2,1,0:T(2,128)S(1)} %get-tuple-element.88), channel_id=1, source_target_pairs={{1,0},{2,1},{3,2},{4,3},{5,4},{6,5},{7,6},{0,7},{9,8},{10,9},{11,1... | collective-permute-start | bytes 221192 | tf_op jit(solution)/shard_map/ppermute | solution.py:35
  479.6 105.4 %collective-permute-start.15 = (f32[3,8,2,384]{3,2,1,0:T(2,128)S(1)}, f32[3,8,2,384]{3,2,1,0:T(2,128)S(1)}, u32[]{:S(2)}, u32[]{:S(2)}) collective-permute-start(f32[3,8,2,384]{3,2,1,0:T(2,128)S(1)} %get-tuple-element.87), channel_id=1, source_target_pairs={{0,1},{1,2},{2,3},{3,4},{4,5},{5,6},{6,7},{7,0},{8,9},{9,10},{10,1... | collective-permute-start | bytes 221192 | tf_op jit(solution)/shard_map/ppermute | solution.py:34
  481.1 104.0 %collective-permute-start.12 = (f32[3,2,64,384]{3,2,1,0:T(8,128)}, f32[3,2,64,384]{3,2,1,0:T(8,128)S(1)}, u32[]{:S(2)}, u32[]{:S(2)}) collective-permute-start(f32[3,2,64,384]{3,2,1,0:T(8,128)} %get-tuple-element.86), channel_id=1, source_target_pairs={{8,0},{16,8},{24,16},{32,24},{40,32},{48,40},{56,48},{64,56},{72,6... | collective-permute-start | bytes 1769480 | tf_op jit(solution)/shard_map/ppermute | solution.py:35
  481.1 104.0 %collective-permute-start.13 = (f32[3,2,64,384]{3,2,1,0:T(8,128)}, f32[3,2,64,384]{3,2,1,0:T(8,128)}, u32[]{:S(2)}, u32[]{:S(2)}) collective-permute-start(f32[3,2,64,384]{3,2,1,0:T(8,128)} %get-tuple-element.85), channel_id=1, source_target_pairs={{0,8},{8,16},{16,24},{24,32},{32,40},{40,48},{48,56},{56,64},{64,7... | collective-permute-start | bytes 1769480 | tf_op jit(solution)/shard_map/ppermute | solution.py:34
  (63 other events, 2092.8 us)
